TPU v7x, 32 devices: a whole 2x2x4 slice. The times are simulated.
32 devices in a mesh: seq: 8 (over z, x), head: 4 (over y, core).
Axes of the slice: x: 2, y: 2, z: 4, core: 2. Of those that a mesh axis runs over, the one named last changes fastest.
Arguments:
- prompt_queries: bfloat16 [1536, 4096], P('seq', 'head'), may hold values from -16 to 16
- prompt_keys: bfloat16 [1536, 1024], P('seq', 'head'), may hold values from -16 to 16
- prompt_values: bfloat16 [1536, 1024], P('seq', 'head'), may hold values from -6 to 6
- span_offset: int32 [8], P('seq'), may hold values from 0 to 7, each once
- appended_queries: bfloat16 [8, 4096], P(None, 'head'), may hold values from -16 to 16
- appended_keys: bfloat16 [8, 1024], P(None, 'head'), may hold values from -6 to 6
- appended_values: bfloat16 [8, 1024], P(None, 'head'), may hold values from -6 to 6
- dec_pos: int32 [8], replicated, may hold values from 2 to 1536, as said below
- out_weight: bfloat16 [4096, 4096], P('head'), may hold values from -0.09375 to 0.09375
Outputs:
- layer_out: bfloat16 [1536, 4096], P(('seq', 'head'))
- dec_out: bfloat16 [8, 4096], P('seq', 'head')
Inputs may be any that keep to these rules, and one draw needn't show every extreme that they name: span_offset is a permutation of 0 to 7. `dec_pos`: some appended token stands at 1536 in every draw.
All inputs are finite; a program needn't handle non-finite values.
Results may differ from a plain program's by a relative error of at most 0.015.
Values may be sent and summed in bfloat16 or wider, within the bound.
A program may use at most 256 MiB of HBM per device.

v0:
```python
import functools
import math

import jax
import jax.numpy as jnp
from jax import lax
from jax.experimental import pallas as pl
from jax.experimental.pallas import tpu as pltpu
from jax.sharding import PartitionSpec as P

QUERY_HEADS = 32
KEY_VALUE_HEADS = 8
HEAD_SIZE = 128
GROUP = QUERY_HEADS // KEY_VALUE_HEADS
MESH = pl.DeviceIdType.MESH

masked_score = -1e30
exp2_scale = HEAD_SIZE ** (-0.5) * math.log2(math.e)


def tiled(column, width):
    return jnp.concatenate([column] * (width // column.shape[1]), axis=1)


def softmax_step(scores, allowed, value_rows, m_ref, l_ref, acc_ref, slot):
    scores = jnp.where(allowed, scores, masked_score)
    old_max = m_ref[slot]
    new_max = jnp.maximum(old_max, jnp.max(scores, axis=1, keepdims=True))
    weights = jnp.exp2((scores - tiled(new_max, scores.shape[1])) * exp2_scale)
    factor = jnp.exp2((old_max - new_max) * exp2_scale)
    m_ref[slot] = new_max
    l_ref[slot] = l_ref[slot] * factor + jnp.sum(weights, axis=1, keepdims=True)
    added = jnp.dot(
        weights.astype(jnp.bfloat16), value_rows, preferred_element_type=jnp.float32
    )
    acc_ref[slot] = acc_ref[slot] * factor + added


def hand_on(layer_in, dec_in, layer_out, dec_out):
    layer_out[...] = layer_in[...]
    dec_out[...] = dec_in[...]


def row_cuts(tok):
    first = max(tok // 96, 1) * 16
    half = (tok - first) // 32 * 16
    return ((0, first), (first, half), (first + half, tok - first - half))


def kernel(
    n_seq, own_dec, chunk,
    q_ref, k_ref, v_ref, span_ref, aq_ref, ak_ref, av_ref, pos_ref, w_hbm,
    out_ref, dec_ref,
    kbuf, vbuf, obuf, wbuf, m_ref, l_ref, acc_ref, md_ref, ld_ref, accd_ref,
    attn, pbuf, own, send1, recv1, send2, recv2, dpart, dsend, drecv,
    local_sem, w_sem, ss, rs, ss1, rs1, ss2, rs2, dss, drs,
):
    tok, width = q_ref.shape
    kv_heads = k_ref.shape[1] // HEAD_SIZE
    n_dec = aq_ref.shape[0]
    model = w_hbm.shape[1]
    part = tok // 4
    line = n_seq // 2
    seq = lax.axis_index("seq")
    head = lax.axis_index("head")
    z, x = seq // 2, seq % 2
    y, c = head // 2, head % 2
    to_x = (2 * z + 1 - x, head)
    to_right = (jnp.minimum(seq + 2, n_seq - 1), head)
    to_left = (jnp.maximum(seq - 2, 0), head)
    to_core = (seq, 2 * y + 1 - c)
    to_y = (seq, 2 * (1 - y) + c)
    to_diag = (seq, 2 * (1 - y) + 1 - c)
    has_left, has_right = z > 0, z < line - 1

    weight_copy = pltpu.make_async_copy(w_hbm, wbuf, w_sem)
    weight_copy.start()
    cuts = row_cuts(tok)
    pieces = [(k_ref, kbuf, cuts[0]), (v_ref, vbuf, cuts[0]), (span_ref, obuf, (0, 8))]
    pieces += [(k_ref, kbuf, cut) for cut in cuts[1:]]
    pieces += [(v_ref, vbuf, cut) for cut in cuts[1:]]
    early, late = (), tuple(range(len(pieces)))
    locals_ = [
        pltpu.make_async_copy(source, buffer.at[seq], local_sem.at[i])
        for i, (source, buffer) in enumerate(
            ((span_ref, obuf), (k_ref, kbuf), (v_ref, vbuf))
        )
    ]
    for copy in locals_:
        copy.start()

    barrier = pltpu.get_barrier_semaphore()
    for peer in (to_x, to_core, to_y, to_diag):
        pl.semaphore_signal(barrier, inc=1, device_id=peer, device_id_type=MESH)
    pl.when(has_left)(
        lambda: pl.semaphore_signal(barrier, inc=1, device_id=to_left, device_id_type=MESH)
    )
    pl.when(has_right)(
        lambda: pl.semaphore_signal(barrier, inc=1, device_id=to_right, device_id_type=MESH)
    )
    pl.semaphore_wait(barrier, 4 + jnp.where(has_left, 1, 0) + jnp.where(has_right, 1, 0))

    targets = (to_left, to_right, to_x)

    def moved(piece, origin, way, first=False):
        source, buffer, (begin, size) = pieces[piece]
        slot = buffer.at[origin, pl.ds(begin, size)]
        return pltpu.make_async_remote_copy(
            src_ref=source.at[pl.ds(begin, size)] if first else slot,
            dst_ref=slot,
            send_sem=ss.at[way, piece, origin],
            recv_sem=rs.at[piece, origin],
            device_id=targets[way],
            device_id_type=MESH,
        )

    def nearest(j):
        reach = jnp.minimum(z, line - 1 - z)
        half = (j + 1) // 2
        both = jnp.where(j % 2 == 1, z - half, z + half)
        single = jnp.where(z < line - 1 - z, z + (j - reach), z - (j - reach))
        return jnp.where(j <= 2 * reach, both, single)

    partner = 2 * z + 1 - x
    for piece in early + late:
        moved(piece, seq, 2, True).start()
        pl.when(has_left)(lambda: moved(piece, seq, 0, True).start())
        pl.when(has_right)(lambda: moved(piece, seq, 1, True).start())

    def dec_rows(ref, h, g=0):
        col = (h * GROUP + g) * HEAD_SIZE if ref is aq_ref else h * HEAD_SIZE
        return ref[:, col : col + HEAD_SIZE].astype(jnp.float32)

    for h in range(kv_heads):
        q32 = jnp.concatenate([dec_rows(aq_ref, h, g) for g in range(GROUP)], axis=0)
        k32 = jnp.concatenate([dec_rows(ak_ref, h)] * GROUP, axis=0)
        v32 = jnp.concatenate([dec_rows(av_ref, h)] * GROUP, axis=0)
        self_score = jnp.sum(q32 * k32, axis=1, keepdims=True)
        md_ref[h] = jnp.broadcast_to(self_score, q32.shape)
        ld_ref[h] = jnp.ones(q32.shape, jnp.float32)
        accd_ref[h] = v32
    m_ref[...] = jnp.full(m_ref.shape, masked_score, jnp.float32)
    l_ref[...] = jnp.zeros(l_ref.shape, jnp.float32)
    acc_ref[...] = jnp.zeros(acc_ref.shape, jnp.float32)
    own_off = span_ref[0:1, 0:1]
    dec_index = lax.broadcasted_iota(jnp.int32, (GROUP * n_dec, 1), 0) % n_dec
    dec_limit = jnp.zeros((GROUP * n_dec, 1), jnp.int32)
    for i in range(n_dec):
        dec_limit = jnp.where(dec_index == i, pos_ref[i], dec_limit)
    for copy in locals_:
        copy.wait()

    for piece in early:
        moved(piece, partner, 2).wait_recv()
        pl.when(has_left)(lambda: moved(piece, partner, 0).start())
        pl.when(has_right)(lambda: moved(piece, partner, 1).start())

    arrivals = [(piece, False) for piece in early + late] + [(piece, True) for piece in early]

    def relay(distance):
        for piece, other in arrivals:
            column = 1 - x if other else x

            @pl.when(z >= distance)
            def _():
                origin = 2 * (z - distance) + column
                moved(piece, origin, 1).wait_recv()
                pl.when(has_right)(lambda: moved(piece, origin, 1).start())
                if piece in late:
                    moved(piece, origin, 2).start()

            @pl.when(z + distance < line)
            def _():
                origin = 2 * (z + distance) + column
                moved(piece, origin, 0).wait_recv()
                pl.when(has_left)(lambda: moved(piece, origin, 0).start())
                if piece in late:
                    moved(piece, origin, 2).start()

    def pair_step(j, carry):
        pl.when(j + 1 < line)(lambda: relay(j + 1))
        zz = nearest(j)
        for piece in late:
            moved(piece, 2 * zz + 1 - x, 2).wait_recv()
        key_id = lax.broadcasted_iota(jnp.int32, (1, 2 * tok), 1)
        first = key_id < tok
        offset = jnp.where(first, obuf[2 * zz][0:1, 0:1], obuf[2 * zz + 1][0:1, 0:1])
        key_pos = offset * tok + jnp.where(first, key_id, key_id - tok)
        query_pos = own_off * tok + lax.broadcasted_iota(jnp.int32, (tok, 1), 0)
        allowed = key_pos <= query_pos
        dec_allowed = key_pos < dec_limit
        for h in range(kv_heads):
            cols = slice(h * HEAD_SIZE, (h + 1) * HEAD_SIZE)
            keys = jnp.concatenate([kbuf[2 * zz, :, cols], kbuf[2 * zz + 1, :, cols]], axis=0)
            vals = jnp.concatenate([vbuf[2 * zz, :, cols], vbuf[2 * zz + 1, :, cols]], axis=0)
            for g in range(GROUP):
                i = h * GROUP + g
                queries = q_ref[:, i * HEAD_SIZE : (i + 1) * HEAD_SIZE]
                scores = lax.dot_general(
                    queries, keys, (((1,), (1,)), ((), ())),
                    preferred_element_type=jnp.float32,
                )
                softmax_step(scores, allowed, vals, m_ref, l_ref, acc_ref, i)
            q32 = jnp.concatenate([dec_rows(aq_ref, h, g) for g in range(GROUP)], axis=0)
            scores = lax.dot_general(
                q32.astype(jnp.bfloat16), keys, (((1,), (1,)), ((), ())),
                preferred_element_type=jnp.float32,
            )
            softmax_step(scores, dec_allowed, vals, md_ref, ld_ref, accd_ref, h)
        return carry

    lax.fori_loop(0, line, pair_step, 0)

    pad = attn.shape[0] - tok - n_dec
    for h in range(kv_heads):
        dec = accd_ref[h] / ld_ref[h]
        for g in range(GROUP):
            i = h * GROUP + g
            cols = slice(i * HEAD_SIZE, (i + 1) * HEAD_SIZE)
            attn[0:tok, cols] = (acc_ref[i] / l_ref[i]).astype(jnp.bfloat16)
            rows = dec[g * n_dec : (g + 1) * n_dec]
            if pad:
                rows = jnp.concatenate([rows, jnp.zeros((pad, HEAD_SIZE), jnp.float32)], axis=0)
            attn[tok:, cols] = rows.astype(jnp.bfloat16)
    weight_copy.wait()

    n_chunk = model // chunk

    def core_copy(i):
        return pltpu.make_async_remote_copy(
            src_ref=send1.at[i], dst_ref=recv1.at[i], send_sem=ss1.at[i], recv_sem=rs1.at[i],
            device_id=to_core, device_id_type=MESH,
        )

    def y_copy(i):
        return pltpu.make_async_remote_copy(
            src_ref=send2.at[i], dst_ref=recv2.at[i], send_sem=ss2.at[i], recv_sem=rs2.at[i],
            device_id=to_y, device_id_type=MESH,
        )

    def block(index):
        return pl.ds(pl.multiple_of(index * part, 8), part)

    def project(i, carry):
        @pl.when(i < n_chunk)
        def _():
            cols = pl.ds(pl.multiple_of(i * chunk, chunk), chunk)
            pbuf[...] = jnp.dot(attn[...], wbuf[:, cols], preferred_element_type=jnp.float32)
            send1[i, 0:part] = pbuf[block(2 * (1 - y) + 1 - c)].astype(jnp.bfloat16)
            send1[i, part:] = pbuf[block(2 * y + 1 - c)].astype(jnp.bfloat16)
            core_copy(i).start()
            own[i, 0:part] = pbuf[block(2 * (1 - y) + c)]
            own[i, part:] = pbuf[block(2 * y + c)]
            dpart[:, cols] = pbuf[tok : tok + n_dec]

        @pl.when(i > 0)
        def _():
            core_copy(i - 1).wait_recv()
            total = own[i - 1, 0:part] + recv1[i - 1, 0:part].astype(jnp.float32)
            send2[i - 1] = total.astype(jnp.bfloat16)
            y_copy(i - 1).start()

        return carry

    lax.fori_loop(0, n_chunk + 1, project, 0)

    quarter = model // 4
    mine = pl.ds(seq * own_dec, own_dec)

    def dec_copy(way, peer):
        return pltpu.make_async_remote_copy(
            src_ref=dsend.at[way], dst_ref=drecv.at[way],
            send_sem=dss.at[way], recv_sem=drs.at[way],
            device_id=peer, device_id_type=MESH,
        )

    dec_copies = []
    for way, peer in enumerate((to_core, to_y, to_diag)):
        cols = pl.ds(pl.multiple_of(peer[1] * quarter, 128), quarter)
        dsend[way] = dpart[mine, cols]
        dec_copies.append(dec_copy(way, peer))
        dec_copies[-1].start()

    def gather_sum(i, carry):
        y_copy(i).wait_recv()
        cols = pl.ds(pl.multiple_of(i * chunk, chunk), chunk)
        total = own[i, part:] + recv1[i, part:].astype(jnp.float32)
        out_ref[:, cols] = (total + recv2[i].astype(jnp.float32)).astype(jnp.bfloat16)
        y_copy(i).wait_send()
        core_copy(i).wait_send()
        return carry

    lax.fori_loop(0, n_chunk, gather_sum, 0)
    for copy in dec_copies:
        copy.wait()
    dec_total = dpart[mine, pl.ds(pl.multiple_of(head * quarter, 128), quarter)]
    dec_ref[...] = (dec_total + drecv[0] + drecv[1] + drecv[2]).astype(jnp.bfloat16)

    def drain(zz, carry):
        for piece, other in arrivals:
            origin = 2 * zz + (1 - x if other else x)
            pl.when((zz <= z) & has_right)(lambda: moved(piece, origin, 1).wait_send())
            pl.when((zz >= z) & has_left)(lambda: moved(piece, origin, 0).wait_send())
            if piece in late:
                moved(piece, origin, 2).wait_send()
        return carry

    for piece in early:
        moved(piece, seq, 2).wait_send()
    lax.fori_loop(0, line, drain, 0)


def on_device(
    prompt_queries, prompt_keys, prompt_values, span_offset,
    appended_queries, appended_keys, appended_values, dec_pos, out_weight,
):
    n_seq = lax.axis_size("seq")
    tok, width = prompt_queries.shape
    kv_width = prompt_keys.shape[1]
    kv_heads = kv_width // HEAD_SIZE
    heads = kv_heads * GROUP
    n_dec = appended_queries.shape[0]
    own_dec = n_dec // n_seq
    model = out_weight.shape[1]
    chunk = 512
    n_chunk = model // chunk
    part = tok // 4
    rows = tok + -(-n_dec // 16) * 16
    span = jnp.broadcast_to(span_offset, (8, 128))
    vmem = pl.BlockSpec(memory_space=pltpu.VMEM)
    f32, b16 = jnp.float32, jnp.bfloat16
    dma = pltpu.SemaphoreType.DMA
    results = pl.pallas_call(
        functools.partial(kernel, n_seq, own_dec, chunk),
        out_shape=(
            jax.ShapeDtypeStruct((part, model), b16),
            jax.ShapeDtypeStruct((own_dec, model // 4), b16),
        ),
        in_specs=[vmem] * 7
        + [pl.BlockSpec(memory_space=pltpu.SMEM), pl.BlockSpec(memory_space=pl.ANY)],
        out_specs=(vmem, vmem),
        scratch_shapes=[
            pltpu.VMEM((n_seq, tok, kv_width), b16),
            pltpu.VMEM((n_seq, tok, kv_width), b16),
            pltpu.VMEM((n_seq, 8, 128), jnp.int32),
            pltpu.VMEM(out_weight.shape, b16),
            pltpu.VMEM((heads, tok, HEAD_SIZE), f32),
            pltpu.VMEM((heads, tok, HEAD_SIZE), f32),
            pltpu.VMEM((heads, tok, HEAD_SIZE), f32),
            pltpu.VMEM((kv_heads, GROUP * n_dec, HEAD_SIZE), f32),
            pltpu.VMEM((kv_heads, GROUP * n_dec, HEAD_SIZE), f32),
            pltpu.VMEM((kv_heads, GROUP * n_dec, HEAD_SIZE), f32),
            pltpu.VMEM((rows, width), b16),
            pltpu.VMEM((rows, chunk), f32),
            pltpu.VMEM((n_chunk, 2 * part, chunk), f32),
            pltpu.VMEM((n_chunk, 2 * part, chunk), b16),
            pltpu.VMEM((n_chunk, 2 * part, chunk), b16),
            pltpu.VMEM((n_chunk, part, chunk), b16),
            pltpu.VMEM((n_chunk, part, chunk), b16),
            pltpu.VMEM((n_dec, model), f32),
            pltpu.VMEM((3, own_dec, model // 4), f32),
            pltpu.VMEM((3, own_dec, model // 4), f32),
            dma((3,)), dma,
            dma((3, 7, n_seq)), dma((7, n_seq)),
            dma((n_chunk,)), dma((n_chunk,)), dma((n_chunk,)), dma((n_chunk,)),
            dma((3,)), dma((3,)),
        ],
        compiler_params=pltpu.CompilerParams(
            collective_id=0, has_side_effects=True, vmem_limit_bytes=60 * 2**20
        ),
    )(
        prompt_queries, prompt_keys, prompt_values, span,
        appended_queries, appended_keys, appended_values, dec_pos, out_weight,
    )
    return pl.pallas_call(
        hand_on,
        out_shape=tuple(jax.ShapeDtypeStruct(r.shape, r.dtype) for r in results),
        in_specs=[vmem] * 2,
        out_specs=(vmem, vmem),
        compiler_params=pltpu.CompilerParams(vmem_limit_bytes=4 * 2**20),
    )(*results)


def solution(mesh):
    in_specs = (
        P("seq", "head"),
        P("seq", "head"),
        P("seq", "head"),
        P("seq"),
        P(None, "head"),
        P(None, "head"),
        P(None, "head"),
        P(),
        P("head", None),
    )
    out_specs = (P(("seq", "head"), None), P("seq", "head"))
    return jax.shard_map(
        on_device, mesh=mesh, in_specs=in_specs, out_specs=out_specs, check_vma=False
    )
```

profile of v0, /device:TPU:0, one launch (start us, length us, event | category | flops | bytes accessed | tf_op | source)
XLA Modules:
  0.0 47.4 jit_solution(4311747969001272148)
XLA Ops:
  1.3 0.6 %broadcast_in_dim.2.span_ref = s32[8,128]{1,0:T(8,128)} broadcast(s32[]{:T(128)} %bitcast.1), dimensions={} | broadcast | bytes 4100 | tf_op jit(solution)/shard_map/broadcast_in_dim | solution.py:329
  1.9 43.0 %shard_map.107 = (bf16[48,4096]{1,0:T(8,128)(2,1)}, bf16[1,1024]{1,0:T(2,128)(2,1)}) custom-call(bf16[192,1024]{1,0:T(8,128)(2,1)} %q_ref.1, bf16[192,256]{1,0:T(8,128)(2,1)} %k_ref.1, bf16[192,256]{1,0:T(8,128)(2,1)} %v_ref.1, s32[8,128]{1,0:T(8,128)} %broadcast_in_dim.2.span_ref, bf16[8,1024]{1,0:T(8,128)(2,1)} %aq_ref.1, bf16[8,256]{1,0:T(8,128)(2,1)} %ak_ref.1, ...), custom_call_target="tpu_custom_call" | custom-call | tf_op jit(solution)/shard_map/pallas_call | solution.py:333
  44.9 0.0 copy-start
  44.9 1.0 %copy-done = bf16[48,4096]{1,0:T(8,128)(2,1)S(1)} copy-done((bf16[48,4096]{1,0:T(8,128)(2,1)S(1)}, bf16[48,4096]{1,0:T(8,128)(2,1)}, u32[]{:S(2)}) %copy-start) | copy-done | bytes 393240
  45.9 0.0 copy-start.1
  45.9 0.7 %copy-done.1 = bf16[1,1024]{1,0:T(2,128)(2,1)S(1)} copy-done((bf16[1,1024]{1,0:T(2,128)(2,1)S(1)}, bf16[1,1024]{1,0:T(2,128)(2,1)}, u32[]{:S(2)}) %copy-start.1) | copy-done | bytes 2072
  46.6 0.8 %shard_map.108 = (bf16[48,4096]{1,0:T(8,128)(2,1)}, bf16[1,1024]{1,0:T(2,128)(2,1)}) custom-call(bf16[48,4096]{1,0:T(8,128)(2,1)S(1)} %copy-done, bf16[1,1024]{1,0:T(2,128)(2,1)S(1)} %copy-done.1), custom_call_target="tpu_custom_call" | custom-call | tf_op jit(solution)/shard_map/pallas_call | solution.py:375
Async XLA Ops:
  44.9 1.0 %copy-start = (bf16[48,4096]{1,0:T(8,128)(2,1)S(1)}, bf16[48,4096]{1,0:T(8,128)(2,1)}, u32[]{:S(2)}) copy-start(bf16[48,4096]{1,0:T(8,128)(2,1)} %get-tuple-element.4.layer_in) | copy-start | bytes 1179652
  45.9 0.7 %copy-start.1 = (bf16[1,1024]{1,0:T(2,128)(2,1)S(1)}, bf16[1,1024]{1,0:T(2,128)(2,1)}, u32[]{:S(2)}) copy-start(bf16[1,1024]{1,0:T(2,128)(2,1)} %get-tuple-element.5.dec_in) | copy-start | bytes 6148
where the time goes:
time: 47.6 us; the launch traced here: 47.4 us
  Pallas kernels  43.8 us (92%)
  local copies, waits for them, and re-layouts  2.27 us (5%)
  between operations  1.29 us (3%)
    pallas_call x1, Pallas kernels, on_device(): pl.pallas_call(functools.partial(kernel, n_seq, own_dec, chunk), out_shap...  43 us
    unnamed x4, local copies, waits for them, and re-layouts  1.67 us

commit v1 on v0

v1 whole, which is shorter than its diff:
```python
import functools
import math

import jax
import jax.numpy as jnp
from jax import lax
from jax.experimental import pallas as pl
from jax.experimental.pallas import tpu as pltpu
from jax.sharding import PartitionSpec as P

QUERY_HEADS = 32
KEY_VALUE_HEADS = 8
HEAD_SIZE = 128
GROUP = QUERY_HEADS // KEY_VALUE_HEADS
MESH = pl.DeviceIdType.MESH
LANES = 128
MARK = 16

masked_score = -1e30
exp2_scale = HEAD_SIZE ** (-0.5) * math.log2(math.e)
LEFT, RIGHT, SIDE = 0, 1, 2


def hand_on(layer_in, dec_in, layer_out, dec_out):
    layer_out[...] = layer_in[...]
    dec_out[...] = dec_in[0 : dec_out.shape[0]].astype(dec_out.dtype)


def in_hbm(array):
    return pltpu.with_memory_space_constraint(array, pltpu.MemorySpace.HBM)


def both(*conditions):
    result = conditions[0]
    for condition in conditions[1:]:
        result = jnp.logical_and(result, condition)
    return result


def kernel(
    n_seq, own_dec, chunk, n_dec, tok,
    q_hbm, k_hbm, v_hbm, span_ref, aq_hbm, ak_hbm, av_hbm, pos_hbm, w_hbm,
    out_ref, dec_ref,
    kbuf, vbuf, wbuf, qs, aq_ref, ak_ref, av_ref, m_ref, l_ref, acc_ref,
    pos_ref, attn, pbuf, own, send1, recv1, send2, recv2, dpart, dsend, drecv,
    kv_sem, q_sem, a_sem, w_sem, ss, rs, ss1, rs1, ss2, rs2, dss, drs,
):
    kv_heads = kbuf.shape[1]
    model = w_hbm.shape[1]
    part = tok // 4
    line = n_seq // 2
    rows = GROUP * tok
    lanes = qs.shape[1]
    dec_lanes = lanes - rows
    f32, b16 = jnp.float32, jnp.bfloat16
    seq = lax.axis_index("seq")
    head = lax.axis_index("head")
    z, x = seq // 2, seq % 2
    y, c = head // 2, head % 2
    partner = 2 * z + 1 - x
    to_x = (partner, head)
    to_right = (jnp.minimum(seq + 2, n_seq - 1), head)
    to_left = (jnp.maximum(seq - 2, 0), head)
    to_core = (seq, 2 * y + 1 - c)
    to_y = (seq, 2 * (1 - y) + c)
    to_diag = (seq, 2 * (1 - y) + 1 - c)
    has_left, has_right = z > 0, z < line - 1
    targets = (to_left, to_right, to_x)

    pieces = [(h, kind) for h in range(kv_heads) for kind in (0, 1)]
    early_head = kv_heads - 1

    def column(ref, i):
        return ref.at[:, pl.ds(i * HEAD_SIZE, HEAD_SIZE)]

    kv_copies = []
    for p, (h, kind) in enumerate(pieces):
        source, buffer = ((k_hbm, kbuf), (v_hbm, vbuf))[kind]
        kv_copies.append(pltpu.make_async_copy(
            column(source, h), buffer.at[seq, h, pl.ds(0, tok)], kv_sem.at[p]
        ))
        kv_copies[-1].start()
    small_copies = [
        pltpu.make_async_copy(source, buffer, a_sem.at[i])
        for i, (source, buffer) in enumerate(
            (
                (pos_hbm, pos_ref), (aq_hbm, aq_ref),
                (ak_hbm, ak_ref), (av_hbm, av_ref),
            )
        )
    ]
    for copy in small_copies:
        copy.start()
    q_copies = []
    for h in range(kv_heads):
        for g in range(GROUP):
            i = h * GROUP + g
            q_copies.append(pltpu.make_async_copy(
                column(q_hbm, i), qs.at[h, pl.ds(g * tok, tok)], q_sem.at[i]
            ))
            q_copies[-1].start()
    weight_copy = pltpu.make_async_copy(w_hbm, wbuf, w_sem)
    weight_copy.start()

    barrier = pltpu.get_barrier_semaphore()
    for peer in (to_x, to_core, to_y, to_diag):
        pl.semaphore_signal(barrier, inc=1, device_id=peer, device_id_type=MESH)
    pl.when(has_left)(
        lambda: pl.semaphore_signal(barrier, inc=1, device_id=to_left, device_id_type=MESH)
    )
    pl.when(has_right)(
        lambda: pl.semaphore_signal(barrier, inc=1, device_id=to_right, device_id_type=MESH)
    )
    own_mark = jnp.full((MARK, LANES), span_ref[0], jnp.int32).astype(f32)
    kbuf[seq, 0, pl.ds(tok, MARK), :] = own_mark.astype(b16)
    own_off = own_mark[0:1, 0:1]
    pl.semaphore_wait(barrier, 4 + jnp.where(has_left, 1, 0) + jnp.where(has_right, 1, 0))

    def moved(p, origin, way):
        h, kind = pieces[p]
        count = tok + MARK if p == 0 else tok
        slot = (kbuf, vbuf)[kind].at[origin, h, pl.ds(0, count)]
        return pltpu.make_async_remote_copy(
            src_ref=slot, dst_ref=slot,
            send_sem=ss.at[way, p, origin], recv_sem=rs.at[p, origin],
            device_id=targets[way], device_id_type=MESH,
        )

    def early(p):
        return pieces[p][0] == early_head

    for p in range(len(pieces)):
        kv_copies[p].wait()
        moved(p, seq, SIDE).start()
        pl.when(has_left)(lambda: moved(p, seq, LEFT).start())
        pl.when(has_right)(lambda: moved(p, seq, RIGHT).start())

    def relay_own(d, p):
        @pl.when(z >= d)
        def _():
            origin = 2 * (z - d) + x
            moved(p, origin, RIGHT).wait_recv()
            pl.when(has_right)(lambda: moved(p, origin, RIGHT).start())
            if early(p):
                pl.when(z != d)(lambda: moved(p, origin, SIDE).start())
            else:
                moved(p, origin, SIDE).start()

        @pl.when(z + d < line)
        def _():
            origin = 2 * (z + d) + x
            moved(p, origin, LEFT).wait_recv()
            pl.when(has_left)(lambda: moved(p, origin, LEFT).start())
            if early(p):
                pl.when(z + d != line - 1)(lambda: moved(p, origin, SIDE).start())
            else:
                moved(p, origin, SIDE).start()

    def relay_partner(p):
        moved(p, partner, SIDE).wait_recv()
        if early(p):
            pl.when(z == 0)(lambda: moved(p, partner, RIGHT).start())
            pl.when(z == line - 1)(lambda: moved(p, partner, LEFT).start())

    def relay_corner(d, p):
        @pl.when(z == d)
        def _():
            moved(p, 1 - x, RIGHT).wait_recv()
            pl.when(has_right)(lambda: moved(p, 1 - x, RIGHT).start())

        @pl.when(z + d == line - 1)
        def _():
            origin = 2 * (line - 1) + 1 - x
            moved(p, origin, LEFT).wait_recv()
            pl.when(has_left)(lambda: moved(p, origin, LEFT).start())

    key_id = lax.broadcasted_iota(jnp.int32, (tok, 1), 0).astype(f32)
    dec_lane = lax.broadcasted_iota(jnp.int32, (1, dec_lanes), 1)
    small_copies[0].wait()
    dec_limit = jnp.zeros((1, dec_lanes), jnp.int32)
    for i in range(n_dec):
        dec_limit = jnp.where(
            jnp.logical_and(dec_lane % n_dec == i, dec_lane < GROUP * n_dec), pos_ref[i], dec_limit
        )
    dec_limit = dec_limit.astype(f32)
    query_row = (lax.broadcasted_iota(jnp.int32, (1, rows), 1) % tok).astype(f32)

    def weigh(block, h, diagonal=False):
        offset = own_off if diagonal else kbuf[block, 0, pl.ds(tok, MARK), :][0:1, 0:1].astype(f32)
        scores = lax.dot_general(
            kbuf[block, h, pl.ds(0, tok), :], qs[h], (((1,), (1,)), ((), ())),
            preferred_element_type=f32,
        )
        dec_seen = offset * tok + key_id < dec_limit
        dec_scores = jnp.where(dec_seen, scores[:, rows:], masked_score)
        scores = scores[:, :rows]
        if diagonal:
            scores = jnp.where(key_id <= query_row, scores, masked_score)
        old = m_ref[h][0:1]
        top = jnp.max(scores, axis=0, keepdims=True)
        new = jnp.maximum(old[:, :rows], top)
        if diagonal:
            used = new
        else:
            seen = offset <= own_off
            new = jnp.where(seen, new, old[:, :rows])
            used = jnp.where(seen, new, -masked_score)
        dec_new = jnp.maximum(old[:, rows:], jnp.max(dec_scores, axis=0, keepdims=True))
        new = jnp.concatenate([new, dec_new], axis=1)
        weights = jnp.concatenate([
            jnp.exp2((scores - used) * exp2_scale),
            jnp.exp2((dec_scores - dec_new) * exp2_scale),
        ], axis=1)
        factor = jnp.exp2((old - new) * exp2_scale)
        m_ref[h] = jnp.broadcast_to(new, m_ref.shape[1:])
        l_ref[h] = l_ref[h] * factor + jnp.sum(weights, axis=0, keepdims=True)
        return weights.astype(b16), factor

    def gather_values(block, h, weights, factor):
        added = lax.dot_general(
            vbuf[block, h], weights, (((0,), (0,)), ((), ())), preferred_element_type=f32
        )
        acc_ref[h] = acc_ref[h] * factor + added

    def attend(block, h, diagonal=False):
        weights, factor = weigh(block, h, diagonal)
        gather_values(block, h, weights, factor)

    for copy in small_copies[1:]:
        copy.wait()
    pad = dec_lanes - GROUP * n_dec
    for h in range(kv_heads):
        q32 = jnp.concatenate([
            aq_ref[:, (h * GROUP + g) * HEAD_SIZE : (h * GROUP + g + 1) * HEAD_SIZE].astype(f32)
            for g in range(GROUP)
        ] + ([jnp.zeros((pad, HEAD_SIZE), f32)] if pad else []), axis=0)
        dec_q = q32.astype(b16)
        qs[h, pl.ds(rows, dec_lanes), :] = dec_q
        cols = slice(h * HEAD_SIZE, (h + 1) * HEAD_SIZE)
        own_lane = lax.broadcasted_iota(jnp.int32, (n_dec, dec_lanes), 1)
        own_token = lax.broadcasted_iota(jnp.int32, (n_dec, dec_lanes), 0)
        mine = jnp.logical_and(own_lane % n_dec == own_token, own_lane < GROUP * n_dec)
        pair_scores = lax.dot_general(
            ak_ref[:, cols], dec_q, (((1,), (1,)), ((), ())), preferred_element_type=f32
        )
        self_score = jnp.sum(jnp.where(mine, pair_scores, 0.0), axis=0, keepdims=True)
        picked = lax.dot_general(
            av_ref[:, cols].astype(f32), mine.astype(f32), (((0,), (0,)), ((), ())),
            preferred_element_type=f32,
        )
        m_ref[h] = jnp.broadcast_to(
            jnp.concatenate([jnp.full((1, rows), masked_score, f32), self_score], axis=1),
            m_ref.shape[1:],
        )
        l_ref[h] = jnp.concatenate(
            [jnp.zeros((8, rows), f32), jnp.ones((8, dec_lanes), f32)], axis=1
        )
        acc_ref[h] = jnp.concatenate([jnp.zeros((HEAD_SIZE, rows), f32), picked], axis=1)
    for h in range(kv_heads):
        for g in range(GROUP):
            q_copies[h * GROUP + g].wait()
        attend(seq, h, diagonal=True)

    def near(d, h):
        pl.when(z >= d)(lambda: attend(2 * (z - d) + x, h))
        pl.when(z + d < line)(lambda: attend(2 * (z + d) + x, h))

    def await_side(d, h):
        for p in (2 * h, 2 * h + 1):
            if h == early_head:
                pl.when(z > d)(lambda: moved(p, 2 * (z - d) + 1 - x, SIDE).wait_recv())
                pl.when(z + d < line - 1)(
                    lambda: moved(p, 2 * (z + d) + 1 - x, SIDE).wait_recv()
                )
            else:
                pl.when(z >= d)(lambda: moved(p, 2 * (z - d) + 1 - x, SIDE).wait_recv())
                pl.when(z + d < line)(lambda: moved(p, 2 * (z + d) + 1 - x, SIDE).wait_recv())

    def across(d, h):
        await_side(d, h)
        pl.when(z >= d)(lambda: attend(2 * (z - d) + 1 - x, h))
        pl.when(z + d < line)(lambda: attend(2 * (z + d) + 1 - x, h))

    corner_k, corner_v = 2 * early_head, 2 * early_head + 1

    for p, (h, kind) in enumerate(pieces):
        relay_own(1, p)
        relay_partner(p)
        if kind == 1:
            near(1, h)
    for h in range(kv_heads - 1):
        attend(partner, h)

    def round_(r, carry):
        for p, (h, kind) in enumerate(pieces):
            relay_own(r, p)
            if p == 1:
                relay_corner(r - 1, corner_k)
            if p == 2:
                relay_corner(r - 1, corner_v)
            if kind == 1:
                near(r, h)
                if p == 1:
                    @pl.when(r == 2)
                    def _():
                        attend(partner, early_head)

                    @pl.when(r > 2)
                    def _():
                        across(r - 2, early_head)
        for h in range(kv_heads - 1):
            across(r - 1, h)
        return carry

    lax.fori_loop(2, line, round_, 0)
    across(line - 2, early_head)
    relay_corner(line - 1, corner_k)
    relay_corner(line - 1, corner_v)
    for h in range(kv_heads - 1):
        await_side(line - 1, h)
    for h in range(kv_heads):
        pl.when(z >= line - 1)(lambda: attend(1 - x, h))
        pl.when(z < 1)(lambda: attend(2 * (line - 1) + 1 - x, h))

    dec_pad = attn.shape[0] - tok - n_dec
    for h in range(kv_heads):
        turned = jnp.transpose(acc_ref[h] * (1.0 / l_ref[h][0:1]))
        for g in range(GROUP):
            i = h * GROUP + g
            cols = slice(i * HEAD_SIZE, (i + 1) * HEAD_SIZE)
            attn[0:tok, cols] = turned[g * tok : (g + 1) * tok].astype(b16)
            dec = turned[rows + g * n_dec : rows + (g + 1) * n_dec]
            if dec_pad:
                dec = jnp.concatenate([dec, jnp.zeros((dec_pad, HEAD_SIZE), f32)], axis=0)
            attn[tok:, cols] = dec.astype(b16)
    weight_copy.wait()

    n_chunk = model // chunk

    def core_copy(i):
        return pltpu.make_async_remote_copy(
            src_ref=send1.at[i], dst_ref=recv1.at[i], send_sem=ss1.at[i], recv_sem=rs1.at[i],
            device_id=to_core, device_id_type=MESH,
        )

    def y_copy(i):
        return pltpu.make_async_remote_copy(
            src_ref=send2.at[i], dst_ref=recv2.at[i], send_sem=ss2.at[i], recv_sem=rs2.at[i],
            device_id=to_y, device_id_type=MESH,
        )

    def block(index):
        return pl.ds(pl.multiple_of(index * part, 8), part)

    def project(i, carry):
        @pl.when(i < n_chunk)
        def _():
            cols = pl.ds(pl.multiple_of(i * chunk, chunk), chunk)
            pbuf[...] = jnp.dot(attn[...], wbuf[:, cols], preferred_element_type=f32)
            send1[i, 0:part] = pbuf[block(2 * (1 - y) + 1 - c)].astype(b16)
            send1[i, part:] = pbuf[block(2 * y + 1 - c)].astype(b16)
            core_copy(i).start()
            own[i, 0:part] = pbuf[block(2 * (1 - y) + c)]
            own[i, part:] = pbuf[block(2 * y + c)]
            dpart[:, cols] = pbuf[tok : tok + n_dec]

        @pl.when(i > 0)
        def _():
            core_copy(i - 1).wait_recv()
            total = own[i - 1, 0:part] + recv1[i - 1, 0:part].astype(f32)
            send2[i - 1] = total.astype(b16)
            y_copy(i - 1).start()

        return carry

    lax.fori_loop(0, n_chunk + 1, project, 0)

    quarter = model // 4
    mine = pl.ds(seq * own_dec, own_dec)

    def dec_copy(way, peer):
        return pltpu.make_async_remote_copy(
            src_ref=dsend.at[way], dst_ref=drecv.at[way],
            send_sem=dss.at[way], recv_sem=drs.at[way],
            device_id=peer, device_id_type=MESH,
        )

    dec_copies = []
    for way, peer in enumerate((to_core, to_y, to_diag)):
        cols = pl.ds(pl.multiple_of(peer[1] * quarter, 128), quarter)
        dsend[way] = dpart[mine, cols]
        dec_copies.append(dec_copy(way, peer))
        dec_copies[-1].start()

    def gather_sum(i, carry):
        y_copy(i).wait_recv()
        cols = pl.ds(pl.multiple_of(i * chunk, chunk), chunk)
        total = own[i, part:] + recv1[i, part:].astype(f32)
        out_ref[:, cols] = (total + recv2[i].astype(f32)).astype(b16)
        y_copy(i).wait_send()
        core_copy(i).wait_send()
        return carry

    lax.fori_loop(0, n_chunk, gather_sum, 0)
    for copy in dec_copies:
        copy.wait()
    dec_total = dpart[mine, pl.ds(pl.multiple_of(head * quarter, 128), quarter)]
    dec_total = dec_total + drecv[0] + drecv[1] + drecv[2]
    dec_ref[...] = jnp.broadcast_to(dec_total, dec_ref.shape)

    def drain(oz, carry):
        origin = 2 * oz + x
        edge = jnp.logical_or(oz == 0, oz == line - 1)
        for p in range(len(pieces)):
            pl.when(both(oz <= z, has_right))(lambda: moved(p, origin, RIGHT).wait_send())
            pl.when(both(oz >= z, has_left))(lambda: moved(p, origin, LEFT).wait_send())
            if early(p):
                pl.when(jnp.logical_or(oz == z, jnp.logical_not(edge)))(
                    lambda: moved(p, origin, SIDE).wait_send()
                )
            else:
                moved(p, origin, SIDE).wait_send()
        return carry

    lax.fori_loop(0, line, drain, 0)
    for p in (corner_k, corner_v):
        pl.when(has_right)(lambda: moved(p, 1 - x, RIGHT).wait_send())
        pl.when(has_left)(lambda: moved(p, 2 * (line - 1) + 1 - x, LEFT).wait_send())


def on_device(
    prompt_queries, prompt_keys, prompt_values, span_offset,
    appended_queries, appended_keys, appended_values, dec_pos, out_weight,
):
    n_seq = lax.axis_size("seq")
    tok, width = prompt_queries.shape
    kv_width = prompt_keys.shape[1]
    kv_heads = kv_width // HEAD_SIZE
    heads = kv_heads * GROUP
    n_dec = appended_queries.shape[0]
    own_dec = n_dec // n_seq
    model = out_weight.shape[1]
    chunk = 512
    n_chunk = model // chunk
    part = tok // 4
    rows = tok + -(-n_dec // 16) * 16
    lanes = GROUP * tok + -(-GROUP * n_dec // LANES) * LANES
    vmem = pl.BlockSpec(memory_space=pltpu.VMEM)
    hbm = pl.BlockSpec(memory_space=pltpu.MemorySpace.HBM)
    smem = pl.BlockSpec(memory_space=pltpu.SMEM)
    f32, b16 = jnp.float32, jnp.bfloat16
    dma = pltpu.SemaphoreType.DMA
    n_piece = 2 * kv_heads
    results = pl.pallas_call(
        functools.partial(kernel, n_seq, own_dec, chunk, n_dec, tok),
        out_shape=(
            jax.ShapeDtypeStruct((part, model), b16),
            jax.ShapeDtypeStruct((8 * own_dec, model // 4), f32),
        ),
        in_specs=[hbm] * 3 + [smem] + [hbm] * 5,
        out_specs=(vmem, vmem),
        scratch_shapes=[
            pltpu.VMEM((n_seq, kv_heads, tok + MARK, HEAD_SIZE), b16),
            pltpu.VMEM((n_seq, kv_heads, tok, HEAD_SIZE), b16),
            pltpu.VMEM(out_weight.shape, b16),
            pltpu.VMEM((kv_heads, lanes, HEAD_SIZE), b16),
            pltpu.VMEM((n_dec, width), b16),
            pltpu.VMEM((n_dec, kv_width), b16),
            pltpu.VMEM((n_dec, kv_width), b16),
            pltpu.VMEM((kv_heads, 8, lanes), f32),
            pltpu.VMEM((kv_heads, 8, lanes), f32),
            pltpu.VMEM((kv_heads, HEAD_SIZE, lanes), f32),
            pltpu.SMEM((n_dec,), jnp.int32),
            pltpu.VMEM((rows, width), b16),
            pltpu.VMEM((rows, chunk), f32),
            pltpu.VMEM((n_chunk, 2 * part, chunk), f32),
            pltpu.VMEM((n_chunk, 2 * part, chunk), b16),
            pltpu.VMEM((n_chunk, 2 * part, chunk), b16),
            pltpu.VMEM((n_chunk, part, chunk), b16),
            pltpu.VMEM((n_chunk, part, chunk), b16),
            pltpu.VMEM((n_dec, model), f32),
            pltpu.VMEM((3, own_dec, model // 4), f32),
            pltpu.VMEM((3, own_dec, model // 4), f32),
            dma((n_piece,)), dma((heads,)), dma((4,)), dma,
            dma((3, n_piece, n_seq)), dma((n_piece, n_seq)),
            dma((n_chunk,)), dma((n_chunk,)), dma((n_chunk,)), dma((n_chunk,)),
            dma((3,)), dma((3,)),
        ],
        compiler_params=pltpu.CompilerParams(
            collective_id=0, has_side_effects=True, vmem_limit_bytes=44 * 2**20
        ),
    )(
        *map(in_hbm, (prompt_queries, prompt_keys, prompt_values)), span_offset,
        *map(in_hbm, (appended_queries, appended_keys, appended_values, dec_pos, out_weight)),
    )
    return pl.pallas_call(
        hand_on,
        out_shape=(
            jax.ShapeDtypeStruct((part, model), b16),
            jax.ShapeDtypeStruct((own_dec, model // 4), b16),
        ),
        in_specs=[vmem] * 2,
        out_specs=(vmem, vmem),
        compiler_params=pltpu.CompilerParams(vmem_limit_bytes=4 * 2**20),
    )(*results)


def solution(mesh):
    in_specs = (
        P("seq", "head"),
        P("seq", "head"),
        P("seq", "head"),
        P("seq"),
        P(None, "head"),
        P(None, "head"),
        P(None, "head"),
        P(),
        P("head", None),
    )
    out_specs = (P(("seq", "head"), None), P("seq", "head"))
    return jax.shard_map(
        on_device, mesh=mesh, in_specs=in_specs, out_specs=out_specs, check_vma=False
    )
```

time: 47.6 us -> 39.6 us (0.83)
  Pallas kernels: 43.8 us -> 38.1 us
  local copies, waits for them, and re-layouts: 2.27 us -> 0 us
    pallas_call x2, Pallas kernels: 43.8 us -> 38.1 us  [the longest x1 37.4 us: on_device(): pl.pallas_call(functools.partial(kernel, n_seq, own_dec, chunk, n_dec, to...]
    unnamed x4 -> x0, local copies, waits for them, and re-layouts: 1.67 us -> none
    broadcast_in_dim x1 -> x0, local copies, waits for them, and re-layouts: 0.59 us -> none  [on_device(): span = jnp.broadcast_to(span_offset, (8, 128))]
where the time goes in v1:
time: 39.6 us; the launch traced here: 39.4 us
  Pallas kernels  38.1 us (96%)
  between operations  1.29 us (3%)
    pallas_call x1, Pallas kernels, on_device(): pl.pallas_call(functools.partial(kernel, n_seq, own_dec, chunk, n_dec, to...  37.4 us

profile of v1, /device:TPU:0, one launch (start us, length us, event | category | flops | bytes accessed | tf_op | source)
XLA Modules:
  0.0 39.4 jit_solution(934640177544244941)
XLA Ops:
  1.3 37.4 %shard_map.104 = (bf16[48,4096]{1,0:T(8,128)(2,1)S(1)}, f32[8,1024]{1,0:T(8,128)S(1)}) custom-call(bf16[192,1024]{1,0:T(8,128)(2,1)} %q_hbm.1, bf16[192,256]{1,0:T(8,128)(2,1)} %k_hbm.1, bf16[192,256]{1,0:T(8,128)(2,1)} %v_hbm.1, s32[1]{0:T(128)S(6)} %copy.11.span_ref, bf16[8,1024]{1,0:T(8,128)(2,1)} %aq_hbm.1, bf16[8,256]{1,0:T(8,128)(2,1)} %ak_hbm.1, ...), custom_call_target="tpu_custom_call" | custom-call | tf_op jit(solution)/shard_map/pallas_call | solution.py:454
  38.6 0.8 %shard_map.105 = (bf16[48,4096]{1,0:T(8,128)(2,1)}, bf16[1,1024]{1,0:T(2,128)(2,1)}) custom-call(bf16[48,4096]{1,0:T(8,128)(2,1)S(1)} %get-tuple-element.4.layer_in, f32[8,1024]{1,0:T(8,128)S(1)} %get-tuple-element.5.dec_in), custom_call_target="tpu_custom_call" | custom-call | tf_op jit(solution)/shard_map/pallas_call | solution.py:496

commit v2 on v1

--- a/solution.py
+++ b/solution.py
@@ -67,6 +67,16 @@
     has_left, has_right = z > 0, z < line - 1
     targets = (to_left, to_right, to_x)
 
+    barrier = pltpu.get_barrier_semaphore()
+    for peer in (to_x, to_core, to_y, to_diag):
+        pl.semaphore_signal(barrier, inc=1, device_id=peer, device_id_type=MESH)
+    pl.when(has_left)(
+        lambda: pl.semaphore_signal(barrier, inc=1, device_id=to_left, device_id_type=MESH)
+    )
+    pl.when(has_right)(
+        lambda: pl.semaphore_signal(barrier, inc=1, device_id=to_right, device_id_type=MESH)
+    )
+
     pieces = [(h, kind) for h in range(kv_heads) for kind in (0, 1)]
     early_head = kv_heads - 1
 
@@ -102,15 +112,6 @@
     weight_copy = pltpu.make_async_copy(w_hbm, wbuf, w_sem)
     weight_copy.start()
 
-    barrier = pltpu.get_barrier_semaphore()
-    for peer in (to_x, to_core, to_y, to_diag):
-        pl.semaphore_signal(barrier, inc=1, device_id=peer, device_id_type=MESH)
-    pl.when(has_left)(
-        lambda: pl.semaphore_signal(barrier, inc=1, device_id=to_left, device_id_type=MESH)
-    )
-    pl.when(has_right)(
-        lambda: pl.semaphore_signal(barrier, inc=1, device_id=to_right, device_id_type=MESH)
-    )
     own_mark = jnp.full((MARK, LANES), span_ref[0], jnp.int32).astype(f32)
     kbuf[seq, 0, pl.ds(tok, MARK), :] = own_mark.astype(b16)
     own_off = own_mark[0:1, 0:1]
@@ -222,9 +223,10 @@
         )
         acc_ref[h] = acc_ref[h] * factor + added
 
-    def attend(block, h, diagonal=False):
-        weights, factor = weigh(block, h, diagonal)
-        gather_values(block, h, weights, factor)
+    def attend(block, diagonal=False):
+        weighed = [weigh(block, h, diagonal) for h in range(kv_heads)]
+        for h in range(kv_heads):
+            gather_values(block, h, *weighed[h])
 
     for copy in small_copies[1:]:
         copy.wait()
@@ -256,14 +258,15 @@
             [jnp.zeros((8, rows), f32), jnp.ones((8, dec_lanes), f32)], axis=1
         )
         acc_ref[h] = jnp.concatenate([jnp.zeros((HEAD_SIZE, rows), f32), picked], axis=1)
-    for h in range(kv_heads):
-        for g in range(GROUP):
-            q_copies[h * GROUP + g].wait()
-        attend(seq, h, diagonal=True)
-
-    def near(d, h):
-        pl.when(z >= d)(lambda: attend(2 * (z - d) + x, h))
-        pl.when(z + d < line)(lambda: attend(2 * (z + d) + x, h))
+    for copy in q_copies:
+        copy.wait()
+    attend(seq, diagonal=True)
+
+    edge = jnp.logical_or(z == 0, z == line - 1)
+
+    def near(d):
+        pl.when(z >= d)(lambda: attend(2 * (z - d) + x))
+        pl.when(z + d < line)(lambda: attend(2 * (z + d) + x))
 
     def await_side(d, h):
         for p in (2 * h, 2 * h + 1):
@@ -276,51 +279,49 @@
                 pl.when(z >= d)(lambda: moved(p, 2 * (z - d) + 1 - x, SIDE).wait_recv())
                 pl.when(z + d < line)(lambda: moved(p, 2 * (z + d) + 1 - x, SIDE).wait_recv())
 
-    def across(d, h):
-        await_side(d, h)
-        pl.when(z >= d)(lambda: attend(2 * (z - d) + 1 - x, h))
-        pl.when(z + d < line)(lambda: attend(2 * (z + d) + 1 - x, h))
+    def across(d):
+        for h in range(kv_heads):
+            await_side(d, h)
+        pl.when(z >= d)(lambda: attend(2 * (z - d) + 1 - x))
+        pl.when(z + d < line)(lambda: attend(2 * (z + d) + 1 - x))
 
     corner_k, corner_v = 2 * early_head, 2 * early_head + 1
 
-    for p, (h, kind) in enumerate(pieces):
+    for p in range(len(pieces)):
         relay_own(1, p)
         relay_partner(p)
-        if kind == 1:
-            near(1, h)
-    for h in range(kv_heads - 1):
-        attend(partner, h)
+    near(1)
 
     def round_(r, carry):
-        for p, (h, kind) in enumerate(pieces):
+        for p in range(len(pieces)):
             relay_own(r, p)
             if p == 1:
                 relay_corner(r - 1, corner_k)
+                pl.when(both(r == 2, edge))(lambda: attend(partner))
+                pl.when(both(r > 2, edge))(lambda: across(r - 2))
             if p == 2:
                 relay_corner(r - 1, corner_v)
-            if kind == 1:
-                near(r, h)
-                if p == 1:
-                    @pl.when(r == 2)
-                    def _():
-                        attend(partner, early_head)
-
-                    @pl.when(r > 2)
-                    def _():
-                        across(r - 2, early_head)
+        near(r)
+        pl.when(both(r == 2, jnp.logical_not(edge)))(lambda: attend(partner))
+        pl.when(both(r > 2, jnp.logical_not(edge)))(lambda: across(r - 2))
+        return carry
+
+    lax.fori_loop(2, line, round_, 0)
+    across(line - 2)
+
+    def finish(origin):
         for h in range(kv_heads - 1):
-            across(r - 1, h)
-        return carry
-
-    lax.fori_loop(2, line, round_, 0)
-    across(line - 2, early_head)
-    relay_corner(line - 1, corner_k)
-    relay_corner(line - 1, corner_v)
-    for h in range(kv_heads - 1):
-        await_side(line - 1, h)
-    for h in range(kv_heads):
-        pl.when(z >= line - 1)(lambda: attend(1 - x, h))
-        pl.when(z < 1)(lambda: attend(2 * (line - 1) + 1 - x, h))
+            moved(2 * h, origin, SIDE).wait_recv()
+        relay_corner(line - 1, corner_k)
+        weighed = [weigh(origin, h) for h in range(kv_heads)]
+        for h in range(kv_heads - 1):
+            moved(2 * h + 1, origin, SIDE).wait_recv()
+        relay_corner(line - 1, corner_v)
+        for h in range(kv_heads):
+            gather_values(origin, h, *weighed[h])
+
+    pl.when(z == line - 1)(lambda: finish(1 - x))
+    pl.when(z == 0)(lambda: finish(2 * (line - 1) + 1 - x))
 
     dec_pad = attn.shape[0] - tok - n_dec
     for h in range(kv_heads):
@@ -336,6 +337,7 @@
     weight_copy.wait()
 
     n_chunk = model // chunk
+    ahead = 2
 
     def core_copy(i):
         return pltpu.make_async_remote_copy(
@@ -352,28 +354,25 @@
     def block(index):
         return pl.ds(pl.multiple_of(index * part, 8), part)
 
+    def pass_on(i):
+        core_copy(i).wait_recv()
+        total = own[i, 0:part] + recv1[i, 0:part].astype(f32)
+        send2[i] = total.astype(b16)
+        y_copy(i).start()
+
     def project(i, carry):
-        @pl.when(i < n_chunk)
-        def _():
-            cols = pl.ds(pl.multiple_of(i * chunk, chunk), chunk)
-            pbuf[...] = jnp.dot(attn[...], wbuf[:, cols], preferred_element_type=f32)
-            send1[i, 0:part] = pbuf[block(2 * (1 - y) + 1 - c)].astype(b16)
-            send1[i, part:] = pbuf[block(2 * y + 1 - c)].astype(b16)
-            core_copy(i).start()
-            own[i, 0:part] = pbuf[block(2 * (1 - y) + c)]
-            own[i, part:] = pbuf[block(2 * y + c)]
-            dpart[:, cols] = pbuf[tok : tok + n_dec]
-
-        @pl.when(i > 0)
-        def _():
-            core_copy(i - 1).wait_recv()
-            total = own[i - 1, 0:part] + recv1[i - 1, 0:part].astype(f32)
-            send2[i - 1] = total.astype(b16)
-            y_copy(i - 1).start()
-
+        cols = pl.ds(pl.multiple_of(i * chunk, chunk), chunk)
+        pbuf[...] = jnp.dot(attn[...], wbuf[:, cols], preferred_element_type=f32)
+        send1[i, 0:part] = pbuf[block(2 * (1 - y) + 1 - c)].astype(b16)
+        send1[i, part:] = pbuf[block(2 * y + 1 - c)].astype(b16)
+        core_copy(i).start()
+        own[i, 0:part] = pbuf[block(2 * (1 - y) + c)]
+        own[i, part:] = pbuf[block(2 * y + c)]
+        dpart[:, cols] = pbuf[tok : tok + n_dec]
+        pl.when(i >= ahead)(lambda: pass_on(i - ahead))
         return carry
 
-    lax.fori_loop(0, n_chunk + 1, project, 0)
+    lax.fori_loop(0, n_chunk, project, 0)
 
     quarter = model // 4
     mine = pl.ds(seq * own_dec, own_dec)
@@ -392,21 +391,8 @@
         dec_copies.append(dec_copy(way, peer))
         dec_copies[-1].start()
 
-    def gather_sum(i, carry):
-        y_copy(i).wait_recv()
-        cols = pl.ds(pl.multiple_of(i * chunk, chunk), chunk)
-        total = own[i, part:] + recv1[i, part:].astype(f32)
-        out_ref[:, cols] = (total + recv2[i].astype(f32)).astype(b16)
-        y_copy(i).wait_send()
-        core_copy(i).wait_send()
-        return carry
-
-    lax.fori_loop(0, n_chunk, gather_sum, 0)
-    for copy in dec_copies:
-        copy.wait()
-    dec_total = dpart[mine, pl.ds(pl.multiple_of(head * quarter, 128), quarter)]
-    dec_total = dec_total + drecv[0] + drecv[1] + drecv[2]
-    dec_ref[...] = jnp.broadcast_to(dec_total, dec_ref.shape)
+    for i in range(n_chunk - ahead, n_chunk):
+        pass_on(i)
 
     def drain(oz, carry):
         origin = 2 * oz + x
@@ -426,6 +412,22 @@
     for p in (corner_k, corner_v):
         pl.when(has_right)(lambda: moved(p, 1 - x, RIGHT).wait_send())
         pl.when(has_left)(lambda: moved(p, 2 * (line - 1) + 1 - x, LEFT).wait_send())
+
+    def gather_sum(i, carry):
+        y_copy(i).wait_recv()
+        cols = pl.ds(pl.multiple_of(i * chunk, chunk), chunk)
+        total = own[i, part:] + recv1[i, part:].astype(f32)
+        out_ref[:, cols] = (total + recv2[i].astype(f32)).astype(b16)
+        y_copy(i).wait_send()
+        core_copy(i).wait_send()
+        return carry
+
+    lax.fori_loop(0, n_chunk, gather_sum, 0)
+    for copy in dec_copies:
+        copy.wait()
+    dec_total = dpart[mine, pl.ds(pl.multiple_of(head * quarter, 128), quarter)]
+    dec_total = dec_total + drecv[0] + drecv[1] + drecv[2]
+    dec_ref[...] = jnp.broadcast_to(dec_total, dec_ref.shape)
 
 
 def on_device(

time: 39.6 us -> 38.4 us (0.970)
  Pallas kernels: 38.1 us -> 36.9 us
    pallas_call x1, Pallas kernels: 37.4 us -> 36.1 us  [on_device(): pl.pallas_call(functools.partial(kernel, n_seq, own_dec, chunk, n_dec, to...]
where the time goes in v2:
time: 38.4 us; the launch traced here: 38.2 us
  Pallas kernels  36.9 us (96%)
  between operations  1.29 us (3%)
    pallas_call x1, Pallas kernels, on_device(): pl.pallas_call(functools.partial(kernel, n_seq, own_dec, chunk, n_dec, to...  36.1 us
    pallas_call x1, Pallas kernels, on_device(): pl.pallas_call(hand_on, out_shape=(jax.ShapeDtypeStruct((part, model), b1...  0.77 us

profile of v2, /device:TPU:0, one launch (start us, length us, event | category | flops | bytes accessed | tf_op | source)
XLA Modules:
  0.0 38.2 jit_solution(1335488912119672007)
XLA Ops:
  1.3 36.1 %shard_map.104 = (bf16[48,4096]{1,0:T(8,128)(2,1)S(1)}, f32[8,1024]{1,0:T(8,128)S(1)}) custom-call(bf16[192,1024]{1,0:T(8,128)(2,1)} %q_hbm.1, bf16[192,256]{1,0:T(8,128)(2,1)} %k_hbm.1, bf16[192,256]{1,0:T(8,128)(2,1)} %v_hbm.1, s32[1]{0:T(128)S(6)} %copy.11.span_ref, bf16[8,1024]{1,0:T(8,128)(2,1)} %aq_hbm.1, bf16[8,256]{1,0:T(8,128)(2,1)} %ak_hbm.1, ...), custom_call_target="tpu_custom_call" | custom-call | tf_op jit(solution)/shard_map/pallas_call | solution.py:456
  37.4 0.8 %shard_map.105 = (bf16[48,4096]{1,0:T(8,128)(2,1)}, bf16[1,1024]{1,0:T(2,128)(2,1)}) custom-call(bf16[48,4096]{1,0:T(8,128)(2,1)S(1)} %get-tuple-element.4.layer_in, f32[8,1024]{1,0:T(8,128)S(1)} %get-tuple-element.5.dec_in), custom_call_target="tpu_custom_call" | custom-call | tf_op jit(solution)/shard_map/pallas_call | solution.py:498

commit v3 on v2

--- a/solution.py
+++ b/solution.py
@@ -42,8 +42,9 @@
     q_hbm, k_hbm, v_hbm, span_ref, aq_hbm, ak_hbm, av_hbm, pos_hbm, w_hbm,
     out_ref, dec_ref,
     kbuf, vbuf, wbuf, qs, aq_ref, ak_ref, av_ref, m_ref, l_ref, acc_ref,
-    pos_ref, attn, pbuf, own, send1, recv1, send2, recv2, dpart, dsend, drecv,
-    kv_sem, q_sem, a_sem, w_sem, ss, rs, ss1, rs1, ss2, rs2, dss, drs,
+    pos_ref, attn, pbuf, own, send1, recv1, send2, recv2,
+    xown, xsend, xrecv, dpart, dsend, drecv,
+    kv_sem, q_sem, a_sem, w_sem, ss, rs, ss1, rs1, ss2, rs2, dss, drs, xss, xrs,
 ):
     kv_heads = kbuf.shape[1]
     model = w_hbm.shape[1]
@@ -130,9 +131,11 @@
     def early(p):
         return pieces[p][0] == early_head
 
+    for copy in kv_copies:
+        copy.wait()
+    sideways = [(p + 2) % len(pieces) for p in range(len(pieces))]
     for p in range(len(pieces)):
-        kv_copies[p].wait()
-        moved(p, seq, SIDE).start()
+        moved(sideways[p], seq, SIDE).start()
         pl.when(has_left)(lambda: moved(p, seq, LEFT).start())
         pl.when(has_right)(lambda: moved(p, seq, RIGHT).start())
 
@@ -289,7 +292,7 @@
 
     for p in range(len(pieces)):
         relay_own(1, p)
-        relay_partner(p)
+        relay_partner(sideways[p])
     near(1)
 
     def round_(r, carry):
@@ -336,7 +339,8 @@
             attn[tok:, cols] = dec.astype(b16)
     weight_copy.wait()
 
-    n_chunk = model // chunk
+    direct = xown.shape[1]
+    n_chunk = (model - direct) // chunk
     ahead = 2
 
     def core_copy(i):
@@ -353,6 +357,25 @@
 
     def block(index):
         return pl.ds(pl.multiple_of(index * part, 8), part)
+
+    def columns(i):
+        return pl.ds(pl.multiple_of(direct + i * chunk, LANES), chunk)
+
+    first = slice(0, direct)
+    pbuf[:, first] = jnp.dot(attn[...], wbuf[:, first], preferred_element_type=f32)
+    first_copies = []
+    for way, (peer, owner) in enumerate((
+        (to_y, 2 * (1 - y) + c), (to_diag, 2 * (1 - y) + 1 - c), (to_core, 2 * y + 1 - c),
+    )):
+        xsend[way] = pbuf[block(owner), first].astype(b16)
+        first_copies.append(pltpu.make_async_remote_copy(
+            src_ref=xsend.at[way], dst_ref=xrecv.at[way],
+            send_sem=xss.at[way], recv_sem=xrs.at[way],
+            device_id=peer, device_id_type=MESH,
+        ))
+        first_copies[-1].start()
+    xown[...] = pbuf[block(2 * y + c), first]
+    dpart[:, first] = pbuf[tok : tok + n_dec, first]
 
     def pass_on(i):
         core_copy(i).wait_recv()
@@ -361,14 +384,14 @@
         y_copy(i).start()
 
     def project(i, carry):
-        cols = pl.ds(pl.multiple_of(i * chunk, chunk), chunk)
-        pbuf[...] = jnp.dot(attn[...], wbuf[:, cols], preferred_element_type=f32)
-        send1[i, 0:part] = pbuf[block(2 * (1 - y) + 1 - c)].astype(b16)
-        send1[i, part:] = pbuf[block(2 * y + 1 - c)].astype(b16)
+        cols = columns(i)
+        pbuf[:, 0:chunk] = jnp.dot(attn[...], wbuf[:, cols], preferred_element_type=f32)
+        send1[i, 0:part] = pbuf[block(2 * (1 - y) + 1 - c), 0:chunk].astype(b16)
+        send1[i, part:] = pbuf[block(2 * y + 1 - c), 0:chunk].astype(b16)
         core_copy(i).start()
-        own[i, 0:part] = pbuf[block(2 * (1 - y) + c)]
-        own[i, part:] = pbuf[block(2 * y + c)]
-        dpart[:, cols] = pbuf[tok : tok + n_dec]
+        own[i, 0:part] = pbuf[block(2 * (1 - y) + c), 0:chunk]
+        own[i, part:] = pbuf[block(2 * y + c), 0:chunk]
+        dpart[:, cols] = pbuf[tok : tok + n_dec, 0:chunk]
         pl.when(i >= ahead)(lambda: pass_on(i - ahead))
         return carry
 
@@ -415,13 +438,19 @@
 
     def gather_sum(i, carry):
         y_copy(i).wait_recv()
-        cols = pl.ds(pl.multiple_of(i * chunk, chunk), chunk)
+        cols = columns(i)
         total = own[i, part:] + recv1[i, part:].astype(f32)
         out_ref[:, cols] = (total + recv2[i].astype(f32)).astype(b16)
         y_copy(i).wait_send()
         core_copy(i).wait_send()
         return carry
 
+    for copy in first_copies:
+        copy.wait()
+    total = xown[...]
+    for way in range(3):
+        total = total + xrecv[way].astype(f32)
+    out_ref[:, first] = total.astype(b16)
     lax.fori_loop(0, n_chunk, gather_sum, 0)
     for copy in dec_copies:
         copy.wait()
@@ -442,8 +471,9 @@
     n_dec = appended_queries.shape[0]
     own_dec = n_dec // n_seq
     model = out_weight.shape[1]
-    chunk = 512
-    n_chunk = model // chunk
+    direct = 4 * LANES
+    chunk = next(c for c in (512, 384, 256, LANES) if (model - direct) % c == 0)
+    n_chunk = (model - direct) // chunk
     part = tok // 4
     rows = tok + -(-n_dec // 16) * 16
     lanes = GROUP * tok + -(-GROUP * n_dec // LANES) * LANES
@@ -474,19 +504,22 @@
             pltpu.VMEM((kv_heads, HEAD_SIZE, lanes), f32),
             pltpu.SMEM((n_dec,), jnp.int32),
             pltpu.VMEM((rows, width), b16),
-            pltpu.VMEM((rows, chunk), f32),
+            pltpu.VMEM((rows, max(chunk, direct)), f32),
             pltpu.VMEM((n_chunk, 2 * part, chunk), f32),
             pltpu.VMEM((n_chunk, 2 * part, chunk), b16),
             pltpu.VMEM((n_chunk, 2 * part, chunk), b16),
             pltpu.VMEM((n_chunk, part, chunk), b16),
             pltpu.VMEM((n_chunk, part, chunk), b16),
+            pltpu.VMEM((part, direct), f32),
+            pltpu.VMEM((3, part, direct), b16),
+            pltpu.VMEM((3, part, direct), b16),
             pltpu.VMEM((n_dec, model), f32),
             pltpu.VMEM((3, own_dec, model // 4), f32),
             pltpu.VMEM((3, own_dec, model // 4), f32),
             dma((n_piece,)), dma((heads,)), dma((4,)), dma,
             dma((3, n_piece, n_seq)), dma((n_piece, n_seq)),
             dma((n_chunk,)), dma((n_chunk,)), dma((n_chunk,)), dma((n_chunk,)),
-            dma((3,)), dma((3,)),
+            dma((3,)), dma((3,)), dma((3,)), dma((3,)),
         ],
         compiler_params=pltpu.CompilerParams(
             collective_id=0, has_side_effects=True, vmem_limit_bytes=44 * 2**20

time: 38.4 us -> 37.8 us (0.984)
  Pallas kernels: 36.9 us -> 36.3 us
    pallas_call x1, Pallas kernels: 36.1 us -> 35.6 us  [on_device(): pl.pallas_call(functools.partial(kernel, n_seq, own_dec, chunk, n_dec, to...]
where the time goes in v3:
time: 37.8 us; the launch traced here: 37.6 us
  Pallas kernels  36.3 us (96%)
  between operations  1.29 us (3%)
    pallas_call x1, Pallas kernels, on_device(): pl.pallas_call(functools.partial(kernel, n_seq, own_dec, chunk, n_dec, to...  35.6 us
    pallas_call x1, Pallas kernels, on_device(): pl.pallas_call(hand_on, out_shape=(jax.ShapeDtypeStruct((part, model), b1...  0.77 us

profile of v3, /device:TPU:0, one launch (start us, length us, event | category | flops | bytes accessed | tf_op | source)
XLA Modules:
  0.0 37.6 jit_solution(5214903996426145839)
XLA Ops:
  1.3 35.6 %shard_map.104 = (bf16[48,4096]{1,0:T(8,128)(2,1)S(1)}, f32[8,1024]{1,0:T(8,128)S(1)}) custom-call(bf16[192,1024]{1,0:T(8,128)(2,1)} %q_hbm.1, bf16[192,256]{1,0:T(8,128)(2,1)} %k_hbm.1, bf16[192,256]{1,0:T(8,128)(2,1)} %v_hbm.1, s32[1]{0:T(128)S(6)} %copy.11.span_ref, bf16[8,1024]{1,0:T(8,128)(2,1)} %aq_hbm.1, bf16[8,256]{1,0:T(8,128)(2,1)} %ak_hbm.1, ...), custom_call_target="tpu_custom_call" | custom-call | tf_op jit(solution)/shard_map/pallas_call | solution.py:486
  36.8 0.8 %shard_map.105 = (bf16[48,4096]{1,0:T(8,128)(2,1)}, bf16[1,1024]{1,0:T(2,128)(2,1)}) custom-call(bf16[48,4096]{1,0:T(8,128)(2,1)S(1)} %get-tuple-element.4.layer_in, f32[8,1024]{1,0:T(8,128)S(1)} %get-tuple-element.5.dec_in), custom_call_target="tpu_custom_call" | custom-call | tf_op jit(solution)/shard_map/pallas_call | solution.py:531

commit v4 on v3

--- a/solution.py
+++ b/solution.py
@@ -451,12 +451,13 @@
     for way in range(3):
         total = total + xrecv[way].astype(f32)
     out_ref[:, first] = total.astype(b16)
-    lax.fori_loop(0, n_chunk, gather_sum, 0)
+    lax.fori_loop(0, n_chunk - 1, gather_sum, 0)
     for copy in dec_copies:
         copy.wait()
     dec_total = dpart[mine, pl.ds(pl.multiple_of(head * quarter, 128), quarter)]
     dec_total = dec_total + drecv[0] + drecv[1] + drecv[2]
     dec_ref[...] = jnp.broadcast_to(dec_total, dec_ref.shape)
+    gather_sum(n_chunk - 1, 0)
 
 
 def on_device(

time: 37.8 us -> 37.8 us (level)
  no operation moved by 1% of the time
where the time goes in v4:
time: 37.8 us; the launch traced here: 37.6 us
  Pallas kernels  36.3 us (96%)
  between operations  1.29 us (3%)
    pallas_call x1, Pallas kernels, on_device(): pl.pallas_call(functools.partial(kernel, n_seq, own_dec, chunk, n_dec, to...  35.5 us
    pallas_call x1, Pallas kernels, on_device(): pl.pallas_call(hand_on, out_shape=(jax.ShapeDtypeStruct((part, model), b1...  0.77 us

profile of v4, /device:TPU:0, one launch (start us, length us, event | category | flops | bytes accessed | tf_op | source)
XLA Modules:
  0.0 37.6 jit_solution(17210750178143431020)
XLA Ops:
  1.3 35.5 %shard_map.104 = (bf16[48,4096]{1,0:T(8,128)(2,1)S(1)}, f32[8,1024]{1,0:T(8,128)S(1)}) custom-call(bf16[192,1024]{1,0:T(8,128)(2,1)} %q_hbm.1, bf16[192,256]{1,0:T(8,128)(2,1)} %k_hbm.1, bf16[192,256]{1,0:T(8,128)(2,1)} %v_hbm.1, s32[1]{0:T(128)S(6)} %copy.11.span_ref, bf16[8,1024]{1,0:T(8,128)(2,1)} %aq_hbm.1, bf16[8,256]{1,0:T(8,128)(2,1)} %ak_hbm.1, ...), custom_call_target="tpu_custom_call" | custom-call | tf_op jit(solution)/shard_map/pallas_call | solution.py:487
  36.8 0.8 %shard_map.105 = (bf16[48,4096]{1,0:T(8,128)(2,1)}, bf16[1,1024]{1,0:T(2,128)(2,1)}) custom-call(bf16[48,4096]{1,0:T(8,128)(2,1)S(1)} %get-tuple-element.4.layer_in, f32[8,1024]{1,0:T(8,128)S(1)} %get-tuple-element.5.dec_in), custom_call_target="tpu_custom_call" | custom-call | tf_op jit(solution)/shard_map/pallas_call | solution.py:532
